TPU v7x, 32 devices: a whole 2x2x4 slice. The times are simulated.
32 devices in a mesh: row: 4 (over z), col: 4 (over x, core), depth: 2 (over y).
Axes of the slice: x: 2, y: 2, z: 4, core: 2. Of those that a mesh axis runs over, the one named last changes fastest.
Arguments:
- heads_concat: bfloat16 [2048, 16384], P('row', ('depth', 'col')), may hold values from -6 to 6
- w_out: bfloat16 [16384, 7168], P(('depth', 'row'), 'col'), may hold values from -0.046875 to 0.046875
Outputs:
- projected: bfloat16 [2048, 7168], P('row', ('col', 'depth'))
All inputs are finite; a program needn't handle non-finite values.
Results may differ from a plain program's by a relative error of at most 0.001.
Values may be sent and summed in bfloat16 or wider, within the bound.
A program may use at most 128 MiB of HBM per device.

v0:
```python
import jax
import jax.numpy as jnp
from jax import lax
from jax.sharding import PartitionSpec as P


def per_device(heads_concat, w_out):
    head_half = lax.all_gather(heads_concat, "col", axis=1, tiled=True)
    weight_half = lax.all_gather(w_out, "row", axis=0, tiled=True)
    partial_sum = jnp.dot(head_half, weight_half, preferred_element_type=jnp.float32)
    summed = lax.psum_scatter(partial_sum, "depth", scatter_dimension=1, tiled=True)
    return summed.astype(jnp.bfloat16)


def solution(mesh):
    return jax.shard_map(
        per_device,
        mesh=mesh,
        in_specs=(P("row", ("depth", "col")), P(("depth", "row"), "col")),
        out_specs=P("row", ("col", "depth")),
        check_vma=False,
    )
```

profile of v0, /device:TPU:0, one launch (start us, length us, event | category | flops | bytes accessed | tf_op | source)
XLA Modules:
  0.0 643.9 jit_solution(13111015978111093550)
XLA Ops:
  6.5 0.0 all-gather.3.cloned.1.call-start
  6.5 0.7 all-gather.3.cloned.1.call-update
  7.3 0.0 all-gather.5.cloned.1.call-start
  7.3 0.7 all-gather.5.cloned.1.call-update
  8.0 0.0 reduce-scatter.2.cloned.1.call-start
  8.1 61.9 %all-gather.3.cloned.1.call-done = bf16[512,8192]{1,0:T(8,128)(2,1)} async-done(((bf16[512,2048]{1,0:T(8,128)(2,1)}), bf16[512,8192]{1,0:T(8,128)(2,1)}) %all-gather.3.cloned.1.call-update) | async-done | bytes 8388624 | tf_op jit(solution)/shard_map/all_gather | solution.py:8
  69.9 494.7 %all-gather.5.cloned.1.call-done = bf16[8192,1792]{1,0:T(8,128)(2,1)} async-done(((bf16[2048,1792]{1,0:T(8,128)(2,1)}), bf16[8192,1792]{1,0:T(8,128)(2,1)}) %all-gather.5.cloned.1.call-update) | async-done | bytes 29360144 | tf_op jit(solution)/shard_map/all_gather | solution.py:9
  564.6 22.7 %fusion = f32[512,1792]{1,0:T(8,128)} fusion(bf16[512,8192]{1,0:T(8,128)(2,1)} %all-gather.3.cloned.1.call-done, bf16[8192,1792]{1,0:T(8,128)(2,1)} %all-gather.5.cloned.1.call-done), kind=kOutput, calls=%fused_computation | convolution fusion | flops 15032385536 | bytes 41418752 | tf_op jit(solution)/shard_map/dot_general | solution.py:10
  587.3 0.0 reduce-scatter.2.cloned.1.call-update
  587.3 47.5 %reduce-scatter.2.cloned.1.call-done = f32[512,896]{1,0:T(8,128)} async-done(((f32[512,1792]{1,0:T(8,128)}), f32[512,896]{1,0:T(8,128)}) %reduce-scatter.2.cloned.1.call-update) | async-done | bytes 1835024 | tf_op jit(solution)/shard_map/reduce_scatter | solution.py:11
  634.9 2.5 convert_element_type.3
Async XLA Ops:
  6.5 63.4 %all-gather.3.cloned.1.call-start = ((), (), s32[]{:S(2)}) async-start(), calls=%async_computation.1 | async-start | bytes 10485760 | tf_op jit(solution)/shard_map/all_gather | solution.py:8
  7.3 557.4 %all-gather.5.cloned.1.call-start = ((), (), s32[]{:S(2)}) async-start(), calls=%async_computation.2 | async-start | bytes 36700160 | tf_op jit(solution)/shard_map/all_gather | solution.py:9
  8.0 626.9 %reduce-scatter.2.cloned.1.call-start = ((), (), s32[]{:S(2)}) async-start(), calls=%async_computation.3 | async-start | bytes 5505024 | tf_op jit(solution)/shard_map/reduce_scatter | solution.py:11
Sparse Core Ops, SparseCore 0:
  8.9 60.9 all-gather.2
  71.5 493.0 all-gather.4
  587.4 47.3 reduce-scatter.1
where the time goes:
time: 644 us
  waiting for transfers between devices  606 us (94%)
  matrix products  22.7 us (4%)
  between operations  13.1 us (2%)
    all_gather x1, waiting for transfers between devices, per_device(): weight_half = lax.all_gather(w_out, 'row', axis=0, tiled=True)  495 us
    all_gather x1, waiting for transfers between devices, per_device(): head_half = lax.all_gather(heads_concat, 'col', axis=1, tiled=True)  61.9 us
    reduce_scatter x1, waiting for transfers between devices, per_device(): lax.psum_scatter(partial_sum, 'depth', scatter_dimension=1, tiled=True)  47.5 us
    dot_general x1, matrix products, per_device(): jnp.dot(head_half, weight_half, preferred_element_type=jnp.float32)  22.7 us
  transfers between devices with their start and end apart: 3, of which 3 were waited for; matrix products, arithmetic and copies ran while one was open for 0% of the time, Pallas kernels for 0%

commit v1 on v0

--- a/solution.py
+++ b/solution.py
@@ -5,7 +5,18 @@
 
 
 def per_device(heads_concat, w_out):
-    head_half = lax.all_gather(heads_concat, "col", axis=1, tiled=True)
+    nodes = lax.axis_size("col")
+    block_list = [heads_concat]
+    ii = 0
+    while ii < nodes - 1:
+        latest = lax.ppermute(
+            block_list[-1], "col", [(kk, (kk + 1) % nodes) for kk in range(nodes)]
+        )
+        block_list.append(latest)
+        ii += 1
+    aux = jnp.concatenate(block_list[::-1], 1)
+    opened = lax.axis_index("col")
+    head_half = jnp.roll(aux, (opened + 1) * heads_concat.shape[1], 1)
     weight_half = lax.all_gather(w_out, "row", axis=0, tiled=True)
     partial_sum = jnp.dot(head_half, weight_half, preferred_element_type=jnp.float32)
     summed = lax.psum_scatter(partial_sum, "depth", scatter_dimension=1, tiled=True)

time: 644 us -> 585 us (0.908)
  waiting for transfers between devices: 606 us -> 523 us
  local copies, waits for them, and re-layouts: 0 us -> 21.7 us
    all_gather x1, waiting for transfers between devices: 495 us -> 398 us  [per_device(): weight_half = lax.all_gather(w_out, 'row', axis=0, tiled=True)]
    ppermute x0 -> x3, waiting for transfers between devices: none -> 77.1 us  [per_device(): lax.ppermute(block_list[-1], 'col', [(kk, (kk + 1) % nodes) for kk in ran...]
    all_gather x1 -> x0, waiting for transfers between devices: 61.9 us -> none  [per_device(): head_half = lax.all_gather(heads_concat, 'col', axis=1, tiled=True)]
    unnamed x0 -> x13, local copies, waits for them, and re-layouts: none -> 20.2 us
  transfers between devices with their start and end apart: 3 -> 5, of which waited for: 3 -> 5; matrix products, arithmetic and copies ran while one was open for 0% -> 3% of each run, Pallas kernels for 0% -> 0%
where the time goes in v1:
time: 585 us; the launch traced here: 584 us
  waiting for transfers between devices  523 us (89%)
  matrix products  22.7 us (4%)
  local copies, waits for them, and re-layouts  21.7 us (4%)
  between operations  13.4 us (2%)
    all_gather x1, waiting for transfers between devices, per_device(): weight_half = lax.all_gather(w_out, 'row', axis=0, tiled=True)  398 us
    ppermute x3, waiting for transfers between devices, per_device(): lax.ppermute(block_list[-1], 'col', [(kk, (kk + 1) % nodes) for kk in ran...  77.1 us
    reduce_scatter x1, waiting for transfers between devices, per_device(): lax.psum_scatter(partial_sum, 'depth', scatter_dimension=1, tiled=True)  47.5 us
    dot_general x1, matrix products, per_device(): jnp.dot(head_half, weight_half, preferred_element_type=jnp.float32)  22.7 us
    unnamed x13, local copies, waits for them, and re-layouts  20.2 us
  transfers between devices with their start and end apart: 5, of which 5 were waited for; matrix products, arithmetic and copies ran while one was open for 3% of the time, Pallas kernels for 0%

profile of v1, /device:TPU:0, one launch (start us, length us, event | category | flops | bytes accessed | tf_op | source)
XLA Modules:
  0.0 584.4 jit_solution(342763510306701381)
XLA Ops:
  6.5 0.0 copy-start
  6.5 0.0 all-gather.2.cloned.1.call-start
  6.5 0.7 all-gather.2.cloned.1.call-update
  7.3 0.0 reduce-scatter.2.cloned.1.call-start
  7.3 0.5 collective-permute-start
  7.8 25.8 %collective-permute-done = bf16[512,2048]{1,0:T(8,128)(2,1)S(1)} collective-permute-done((bf16[512,2048]{1,0:T(8,128)(2,1)}, bf16[512,2048]{1,0:T(8,128)(2,1)S(1)}, u32[]{:S(2)}, u32[]{:S(2)}) %collective-permute-start) | collective-permute-done | bytes 2097184 | tf_op jit(solution)/shard_map/ppermute | solution.py:12
  33.7 0.0 copy-start.1
  33.7 1.4 copy-done.1
  35.0 0.0 collective-permute-start.1
  35.1 25.5 %collective-permute-done.1 = bf16[512,2048]{1,0:T(8,128)(2,1)} collective-permute-done((bf16[512,2048]{1,0:T(8,128)(2,1)S(1)}, bf16[512,2048]{1,0:T(8,128)(2,1)}, u32[]{:S(2)}, u32[]{:S(2)}) %collective-permute-start.1) | collective-permute-done | bytes 2097184 | tf_op jit(solution)/shard_map/ppermute | solution.py:12
  60.6 0.0 collective-permute-start.2
  60.6 0.0 copy-start.2
  60.6 25.8 %collective-permute-done.2 = bf16[512,2048]{1,0:T(8,128)(2,1)} collective-permute-done((bf16[512,2048]{1,0:T(8,128)(2,1)}, bf16[512,2048]{1,0:T(8,128)(2,1)}, u32[]{:S(2)}, u32[]{:S(2)}) %collective-permute-start.2) | collective-permute-done | bytes 2097184 | tf_op jit(solution)/shard_map/ppermute | solution.py:12
  86.4 3.2 constant_dynamic-update-slice_fusion.7
  89.5 3.2 constant_dynamic-update-slice_fusion.6
  92.7 3.2 constant_dynamic-update-slice_fusion.5
  95.9 0.0 copy-done
  95.9 1.5 constant_dynamic-update-slice_fusion.4
  97.5 3.2 constant_dynamic-update-slice_fusion.3
  100.6 3.1 constant_dynamic-update-slice_fusion.2
  103.8 0.0 copy-done.2
  103.8 1.4 constant_dynamic-update-slice_fusion.1
  105.2 1.6 constant_dynamic-update-slice_fusion
  106.8 398.0 %all-gather.2.cloned.1.call-done = bf16[8192,1792]{1,0:T(8,128)(2,1)} async-done(((bf16[2048,1792]{1,0:T(8,128)(2,1)}), bf16[8192,1792]{1,0:T(8,128)(2,1)}) %all-gather.2.cloned.1.call-update) | async-done | bytes 29360144 | tf_op jit(solution)/shard_map/all_gather | solution.py:20
  504.8 22.7 %fusion = f32[512,1792]{1,0:T(8,128)} fusion(bf16[8192,1792]{1,0:T(8,128)(2,1)} %all-gather.2.cloned.1.call-done, bf16[512,16384]{1,0:T(8,128)(2,1)} %constant_dynamic-update-slice_fusion, s32[]{:T(128)S(6)} %select_n.14), kind=kOutput, calls=%fused_computation | convolution fusion | flops 15032385536 | bytes 41418756 | tf_op jit(solution)/shard_map/dot_general | solution.py:21
  527.4 0.0 reduce-scatter.2.cloned.1.call-update
  527.5 47.5 %reduce-scatter.2.cloned.1.call-done = f32[512,896]{1,0:T(8,128)} async-done(((f32[512,1792]{1,0:T(8,128)}), f32[512,896]{1,0:T(8,128)}) %reduce-scatter.2.cloned.1.call-update) | async-done | bytes 1835024 | tf_op jit(solution)/shard_map/reduce_scatter | solution.py:22
  575.0 2.5 convert_element_type.3
Async XLA Ops:
  6.5 89.4 %copy-start = (bf16[512,2048]{1,0:T(8,128)(2,1)S(1)}, bf16[512,2048]{1,0:T(8,128)(2,1)}, u32[]{:S(2)}) copy-start(bf16[512,2048]{1,0:T(8,128)(2,1)} %param.2) | copy-start | bytes 6291460
  6.5 498.2 %all-gather.2.cloned.1.call-start = ((), (), s32[]{:S(2)}) async-start(), calls=%async_computation.1 | async-start | bytes 36700160 | tf_op jit(solution)/shard_map/all_gather | solution.py:20
  7.3 567.7 %reduce-scatter.2.cloned.1.call-start = ((), (), s32[]{:S(2)}) async-start(), calls=%async_computation.2 | async-start | bytes 5505024 | tf_op jit(solution)/shard_map/reduce_scatter | solution.py:22
  7.3 26.4 %collective-permute-start = (bf16[512,2048]{1,0:T(8,128)(2,1)}, bf16[512,2048]{1,0:T(8,128)(2,1)S(1)}, u32[]{:S(2)}, u32[]{:S(2)}) collective-permute-start(bf16[512,2048]{1,0:T(8,128)(2,1)} %param.2), channel_id=1, source_target_pairs={{0,2},{2,4},{4,6},{6,0},{1,3},{3,5},{5,7},{7,1},{8,10},{10,12},{12... | collective-permute-start | bytes 6291464 | tf_op jit(solution)/shard_map/ppermute | solution.py:12
  33.7 1.4 copy-start.1
  35.0 25.6 %collective-permute-start.1 = (bf16[512,2048]{1,0:T(8,128)(2,1)S(1)}, bf16[512,2048]{1,0:T(8,128)(2,1)}, u32[]{:S(2)}, u32[]{:S(2)}) collective-permute-start(bf16[512,2048]{1,0:T(8,128)(2,1)S(1)} %collective-permute-done), channel_id=1, source_target_pairs={{0,2},{2,4},{4,6},{6,0},{1,3},{3,5},{5,7},{7,1},{8,10},{10,12},{12... | collective-permute-start | bytes 6291464 | tf_op jit(solution)/shard_map/ppermute | solution.py:12
  60.6 25.8 %collective-permute-start.2 = (bf16[512,2048]{1,0:T(8,128)(2,1)}, bf16[512,2048]{1,0:T(8,128)(2,1)}, u32[]{:S(2)}, u32[]{:S(2)}) collective-permute-start(bf16[512,2048]{1,0:T(8,128)(2,1)} %collective-permute-done.1), channel_id=1, source_target_pairs={{0,2},{2,4},{4,6},{6,0},{1,3},{3,5},{5,7},{7,1},{8,10},{10,12},{12... | collective-permute-start | bytes 6291464 | tf_op jit(solution)/shard_map/ppermute | solution.py:12
  60.6 43.1 %copy-start.2 = (bf16[512,2048]{1,0:T(8,128)(2,1)S(1)}, bf16[512,2048]{1,0:T(8,128)(2,1)}, u32[]{:S(2)}) copy-start(bf16[512,2048]{1,0:T(8,128)(2,1)} %copy-done.1) | copy-start | bytes 6291460
Sparse Core Ops, SparseCore 0:
  8.9 495.8 all-gather.1
  527.6 47.3 reduce-scatter.1
